TPU v7x, 32 devices: a whole 2x2x4 slice. The times are simulated.
32 devices in a mesh: shard: 16 (over z, y, core), model: 2 (over x).
Axes of the slice: x: 2, y: 2, z: 4, core: 2. Of those that a mesh axis runs over, the one named last changes fastest.
Arguments:
- gradients: float32 [128, 128, 4096], P(None, 'shard', 'model'), may hold values from -6 to 6
- momentum: float32 [128, 128, 4096], P(None, 'shard', 'model'), may hold values from -6 to 6
- weights: float32 [128, 128, 4096], P(None, 'shard', 'model'), may hold values from -0.1875 to 0.1875
Outputs:
- new_weights: float32 [128, 128, 4096], P(None, 'shard', 'model')
- new_momentum: float32 [128, 128, 4096], P(None, 'shard', 'model')
All inputs are finite; a program needn't handle non-finite values.
Results may differ from a plain program's by a relative error of at most 0.00012.
Values sent between devices are 32-bit elements; how exact they have to be, the bound alone decides.
A program may use at most 128 MiB of HBM per device.

v0:
```python
import jax
import jax.numpy as jnp
from jax import lax
from jax.sharding import PartitionSpec as P

ITERS = 4
hold_rate = 0.9
learn_rate = 0.8


def local(gradients, momentum, weights):
    new_momentum = hold_rate * momentum + gradients
    direction = hold_rate * new_momentum + gradients
    moved = lax.all_to_all(direction, "shard", split_axis=0, concat_axis=1, tiled=True)
    total = lax.psum(jnp.sum(moved * moved, axis=(1, 2), keepdims=True), "model")
    iterate = moved * lax.rsqrt(total + 1e-06)
    for step in range(ITERS):
        gram = lax.psum(
            jnp.einsum("mik,mjk->mij", iterate, iterate, precision=lax.Precision.HIGHEST), "model"
        )
        mixed = -4.775 * gram + 2.0315 * jnp.einsum(
            "mij,mjk->mik", gram, gram, precision=lax.Precision.HIGHEST
        )
        iterate = 3.4445 * iterate + jnp.einsum(
            "mij,mjk->mik", mixed, iterate, precision=lax.Precision.HIGHEST
        )
    back = lax.all_to_all(iterate, "shard", split_axis=1, concat_axis=0, tiled=True)
    new_weights = weights - learn_rate * back
    return (new_weights, new_momentum)


def solution(mesh):
    return jax.shard_map(
        local,
        mesh=mesh,
        in_specs=(P(None, "shard", "model"), P(None, "shard", "model"), P(None, "shard", "model")),
        out_specs=(P(None, "shard", "model"), P(None, "shard", "model")),
        check_vma=False,
    )
```

profile of v0, /device:TPU:1, one launch (start us, length us, event | category | flops | bytes accessed | tf_op | source)
XLA Modules:
  0.0 666.5 jit_solution(225198048523611833)
XLA Ops:
  7.2 0.0 all-reduce.5.cloned.1.call-start
  7.2 9.3 %multiply_add_fusion.4 = (f32[128,8,2048]{2,1,0:T(8,128)S(1)}, f32[128,8,2048]{2,1,0:T(8,128)}) fusion(f32[128,8,2048]{2,1,0:T(8,128)} %param.3, f32[128,8,2048]{2,1,0:T(8,128)} %param.4), kind=kLoop, calls=%fused_computation.8 | loop fusion | flops 8388608 | bytes 33554432 | tf_op jit(solution)/shard_map/add | solution.py:13
  16.5 189.7 %all_to_all.27 = f32[128,8,2048]{2,1,0:T(8,128)S(1)} all-to-all(f32[128,8,2048]{2,1,0:T(8,128)S(1)} %get-tuple-element.2), channel_id=1, replica_groups=mesh['shard'=16,'model'=2] {'shard'}, dimensions={0} | all-to-all | bytes 16777216 | tf_op jit(solution)/shard_map/all_to_all | solution.py:14
  206.2 0.0 copy-start
  206.2 3.4 copy-done
  209.5 0.8 fusion
  210.3 4.1 psum.35
  214.4 12.9 %fusion.2 = f32[8,128,128]{2,1,0:T(8,128)} fusion(f32[16,8,8,2048]{3,2,1,0:T(8,128)} %bitcast.44, f32[8]{0:T(128)S(1)} %rsqrt_bitcast_fusion), kind=kOutput, calls=%fused_computation.11 | convolution fusion | flops 3223322624 | bytes 8912928 | tf_op jit(solution)/shard_map/mik,mjk->mij/dot_general | solution.py:19
  227.3 0.0 all-reduce.5.cloned.1.call-update
  227.3 0.0 all-reduce.7.cloned.1.call-start
  227.4 29.3 %all-reduce.5.cloned.1.call-done = f32[8,128,128]{2,1,0:T(8,128)} async-done(((f32[8,128,128]{2,1,0:T(8,128)}), f32[8,128,128]{2,1,0:T(8,128)}) %all-reduce.5.cloned.1.call-update) | async-done | bytes 524304 | tf_op jit(solution)/shard_map/psum | solution.py:18
  256.7 2.1 fusion.8
  258.8 11.7 %multiply_add_fusion.3 = f32[8,128,2048]{2,1,0:T(8,128)S(1)} fusion(f32[16,8,8,2048]{3,2,1,0:T(8,128)} %bitcast.45, f32[8,128,128]{2,1,0:T(8,128)S(1)} %fusion.8, f32[8]{0:T(128)S(1)} %rsqrt_bitcast_fusion), kind=kOutput, calls=%fused_computation.7 | convolution fusion | flops 3229614080 | bytes 17301536 | tf_op jit(solution)/shard_map/mij,mjk->mik/dot_general | solution.py:24
  270.5 0.0 copy-start.1
  270.5 3.4 copy-done.1
  273.9 8.5 %fusion.9 = f32[8,128,128]{2,1,0:T(8,128)} fusion(f32[8,128,2048]{2,1,0:T(8,128)S(1)} %multiply_add_fusion.3), kind=kOutput, calls=%fused_computation.24 | convolution fusion | flops 3221225472 | bytes 8912896 | tf_op jit(solution)/shard_map/mik,mjk->mij/dot_general | solution.py:19
  282.4 0.0 all-reduce.7.cloned.1.call-update
  282.4 0.0 all-reduce.9.cloned.1.call-start
  282.5 28.8 %all-reduce.7.cloned.1.call-done = f32[8,128,128]{2,1,0:T(8,128)} async-done(((f32[8,128,128]{2,1,0:T(8,128)}), f32[8,128,128]{2,1,0:T(8,128)}) %all-reduce.7.cloned.1.call-update) | async-done | bytes 524304 | tf_op jit(solution)/shard_map/psum | solution.py:18
  311.3 2.1 fusion.7
  313.3 14.3 %multiply_add_fusion.2 = f32[8,128,2048]{2,1,0:T(8,128)S(1)} fusion(f32[8,128,2048]{2,1,0:T(8,128)} %copy-done.1, f32[8,128,128]{2,1,0:T(8,128)S(1)} %fusion.7), kind=kOutput, calls=%fused_computation.6 | convolution fusion | flops 3225419776 | bytes 17301504 | tf_op jit(solution)/shard_map/mij,mjk->mik/dot_general | solution.py:24
  327.7 0.0 copy-start.2
  327.7 3.4 copy-done.2
  331.1 8.5 %fusion.10 = f32[8,128,128]{2,1,0:T(8,128)} fusion(f32[8,128,2048]{2,1,0:T(8,128)S(1)} %multiply_add_fusion.2), kind=kOutput, calls=%fused_computation.25 | convolution fusion | flops 3221225472 | bytes 8912896 | tf_op jit(solution)/shard_map/mik,mjk->mij/dot_general | solution.py:19
  339.6 0.0 all-reduce.9.cloned.1.call-update
  339.6 0.0 all-reduce.11.cloned.1.call-start
  339.7 28.8 %all-reduce.9.cloned.1.call-done = f32[8,128,128]{2,1,0:T(8,128)} async-done(((f32[8,128,128]{2,1,0:T(8,128)}), f32[8,128,128]{2,1,0:T(8,128)}) %all-reduce.9.cloned.1.call-update) | async-done | bytes 524304 | tf_op jit(solution)/shard_map/psum | solution.py:18
  368.5 2.1 fusion.6
  370.5 14.1 %multiply_add_fusion.1 = f32[8,128,2048]{2,1,0:T(8,128)S(1)} fusion(f32[8,128,2048]{2,1,0:T(8,128)} %copy-done.2, f32[8,128,128]{2,1,0:T(8,128)S(1)} %fusion.6), kind=kOutput, calls=%fused_computation.5 | convolution fusion | flops 3225419776 | bytes 17301504 | tf_op jit(solution)/shard_map/mij,mjk->mik/dot_general | solution.py:24
  384.7 0.0 copy-start.3
  384.7 3.4 copy-done.3
  388.1 8.5 %fusion.11 = f32[8,128,128]{2,1,0:T(8,128)} fusion(f32[8,128,2048]{2,1,0:T(8,128)S(1)} %multiply_add_fusion.1), kind=kOutput, calls=%fused_computation.26 | convolution fusion | flops 3221225472 | bytes 8912896 | tf_op jit(solution)/shard_map/mik,mjk->mij/dot_general | solution.py:19
  396.6 0.0 all-reduce.11.cloned.1.call-update
  396.6 28.8 %all-reduce.11.cloned.1.call-done = f32[8,128,128]{2,1,0:T(8,128)} async-done(((f32[8,128,128]{2,1,0:T(8,128)}), f32[8,128,128]{2,1,0:T(8,128)}) %all-reduce.11.cloned.1.call-update) | async-done | bytes 524304 | tf_op jit(solution)/shard_map/psum | solution.py:18
  425.4 2.1 fusion.5
  427.5 14.9 %multiply_add_fusion = f32[8,128,2048]{2,1,0:T(8,128)S(1)} fusion(f32[8,128,2048]{2,1,0:T(8,128)} %copy-done.3, f32[8,128,128]{2,1,0:T(8,128)S(1)} %fusion.5), kind=kOutput, calls=%fused_computation.4 | convolution fusion | flops 3225419776 | bytes 17301504 | tf_op jit(solution)/shard_map/mij,mjk->mik/dot_general | solution.py:24
  442.4 4.9 copy.8
  447.2 188.9 %all_to_all.28 = f32[8,128,2048]{2,0,1:T(8,128)S(1)} all-to-all(f32[8,128,2048]{2,0,1:T(8,128)S(1)} %copy.8), channel_id=1, replica_groups=mesh['shard'=16,'model'=2] {'shard'}, dimensions={1} | all-to-all | bytes 16777216 | tf_op jit(solution)/shard_map/all_to_all | solution.py:27
  636.2 1.8 broadcast_multiply_fusion
  638.0 9.7 %copy.9 = f32[16,8,8,2048]{3,2,1,0:T(8,128)} copy(f32[16,8,8,2048]{3,1,2,0:T(8,128)S(1)} %bitcast.46) | data formatting | bytes 16777216 | tf_op jit(solution)/shard_map/mul | solution.py:28
  647.7 11.9 %bitcast_subtract_fusion = f32[128,8,2048]{2,1,0:T(8,128)} fusion(f32[128,8,2048]{2,1,0:T(8,128)} %param.5, f32[16,8,8,2048]{3,2,1,0:T(8,128)} %copy.9), kind=kLoop, calls=%fused_computation.1 | loop fusion | flops 2097152 | bytes 25165824 | tf_op jit(solution)/shard_map/sub | solution.py:28
  (1 shorter events, 0.0 us)
Async XLA Ops:
  7.2 249.5 %all-reduce.5.cloned.1.call-start = ((), (), s32[]{:S(2)}) async-start(), calls=%async_computation.2 | async-start | bytes 1048576 | tf_op jit(solution)/shard_map/psum | solution.py:18
  206.2 3.4 copy-start
  227.3 83.9 %all-reduce.7.cloned.1.call-start = ((), (), s32[]{:S(2)}) async-start(), calls=%async_computation.3 | async-start | bytes 1048576 | tf_op jit(solution)/shard_map/psum | solution.py:18
  270.5 3.4 copy-start.1
  282.4 86.0 %all-reduce.9.cloned.1.call-start = ((), (), s32[]{:S(2)}) async-start(), calls=%async_computation.4 | async-start | bytes 1048576 | tf_op jit(solution)/shard_map/psum | solution.py:18
  327.7 3.4 copy-start.2
  339.6 85.8 %all-reduce.11.cloned.1.call-start = ((), (), s32[]{:S(2)}) async-start(), calls=%async_computation.5 | async-start | bytes 1048576 | tf_op jit(solution)/shard_map/psum | solution.py:18
  384.7 3.4 copy-start.3
Sparse Core Ops, SparseCore 0:
  227.5 29.1 all-reduce.4
  282.6 28.6 all-reduce.6
  339.8 28.6 all-reduce.8
  396.7 28.6 all-reduce.10
where the time goes:
time: 675 us; the launch traced here: 667 us
  blocking collectives  383 us (57%)
  waiting for transfers between devices  116 us (17%)
  matrix products  102 us (15%)
  local copies, waits for them, and re-layouts  28.1 us (4%)
  other arithmetic  23.8 us (4%)
  between operations  14.3 us (2%)
    all_to_all x1, blocking collectives, local(): lax.all_to_all(direction, 'shard', split_axis=0, concat_axis=1, tiled=True)  190 us
    all_to_all x1, blocking collectives, local(): lax.all_to_all(iterate, 'shard', split_axis=1, concat_axis=0, tiled=True)  189 us
    psum x4, waiting for transfers between devices, local(): lax.psum(jnp.einsum('mik,mjk->mij', iterate, iterate, precision=lax.Preci...  116 us
    dot_general x4, matrix products, local(): jnp.einsum('mij,mjk->mik', mixed, iterate, precision=lax.Precision.HIGHEST)  55 us
    dot_general x4, matrix products, local(): jnp.einsum('mik,mjk->mij', iterate, iterate, precision=lax.Precision.HIGH...  38.5 us
    unnamed x8, local copies, waits for them, and re-layouts  13.6 us
  transfers between devices with their start and end apart: 4, of which 4 were waited for; matrix products, arithmetic and copies ran while one was open for 0% of the time, Pallas kernels for 0%

commit v1 on v0

--- a/solution.py
+++ b/solution.py
@@ -11,7 +11,9 @@
 def local(gradients, momentum, weights):
     new_momentum = hold_rate * momentum + gradients
     direction = hold_rate * new_momentum + gradients
-    moved = lax.all_to_all(direction, "shard", split_axis=0, concat_axis=1, tiled=True)
+    shards = jnp.split(direction, lax.axis_size("shard"), axis=0)
+    arrived = lax.all_to_all(jnp.stack(shards), "shard", 0, 0)
+    moved = jnp.concatenate(arrived, axis=1)
     total = lax.psum(jnp.sum(moved * moved, axis=(1, 2), keepdims=True), "model")
     iterate = moved * lax.rsqrt(total + 1e-06)
     for step in range(ITERS):

time: 675 us -> 673 us (level)
    unnamed x8 -> x23, local copies, waits for them, and re-layouts: 13.6 us -> 14.1 us
where the time goes in v1:
time: 673 us; the launch traced here: 667 us
  blocking collectives  383 us (57%)
  waiting for transfers between devices  115 us (17%)
  matrix products  102 us (15%)
  local copies, waits for them, and re-layouts  28.7 us (4%)
  other arithmetic  23.8 us (4%)
  between operations  14.4 us (2%)
    all_to_all x1, blocking collectives, local(): arrived = lax.all_to_all(jnp.stack(shards), 'shard', 0, 0)  190 us
    all_to_all x1, blocking collectives, local(): lax.all_to_all(iterate, 'shard', split_axis=1, concat_axis=0, tiled=True)  189 us
    psum x4, waiting for transfers between devices, local(): lax.psum(jnp.einsum('mik,mjk->mij', iterate, iterate, precision=lax.Preci...  115 us
    dot_general x4, matrix products, local(): jnp.einsum('mij,mjk->mik', mixed, iterate, precision=lax.Precision.HIGHEST)  55.1 us
    dot_general x4, matrix products, local(): jnp.einsum('mik,mjk->mij', iterate, iterate, precision=lax.Precision.HIGH...  38.5 us
    unnamed x23, local copies, waits for them, and re-layouts  14.1 us
  transfers between devices with their start and end apart: 4, of which 4 were waited for; matrix products, arithmetic and copies ran while one was open for 0% of the time, Pallas kernels for 0%

profile of v1, /device:TPU:1, one launch (start us, length us, event | category | flops | bytes accessed | tf_op | source)
XLA Modules:
  0.0 667.3 jit_solution(2204244246811271638)
XLA Ops:
  7.2 0.0 all-reduce.5.cloned.1.call-start
  7.2 9.3 %multiply_add_fusion.4 = (f32[128,8,2048]{2,1,0:T(8,128)S(1)}, f32[128,8,2048]{2,1,0:T(8,128)}) fusion(f32[128,8,2048]{2,1,0:T(8,128)} %param.3, f32[128,8,2048]{2,1,0:T(8,128)} %param.4), kind=kLoop, calls=%fused_computation.7 | loop fusion | flops 8388608 | bytes 33554432 | tf_op jit(solution)/shard_map/add | solution.py:13
  17.2 189.7 %all_to_all.14 = f32[16,8,8,2048]{3,2,1,0:T(8,128)S(1)} all-to-all(f32[16,8,8,2048]{3,2,1,0:T(8,128)S(1)} %fusion.8), channel_id=1, replica_groups=mesh['shard'=16,'model'=2] {'shard'}, dimensions={0} | all-to-all | bytes 16777216 | tf_op jit(solution)/shard_map/all_to_all | solution.py:15
  206.9 0.0 copy-start
  206.9 3.4 copy-done
  210.3 0.8 multiply_reduce_fusion
  211.1 4.1 psum.35
  215.1 12.9 %fusion.1 = f32[8,128,128]{2,1,0:T(8,128)} fusion(f32[8]{0:T(128)S(1)} %rsqrt_bitcast_fusion, f32[16,8,8,2048]{3,2,1,0:T(8,128)} %copy-done), kind=kOutput, calls=%fused_computation.10 | convolution fusion | flops 3223322624 | bytes 8912928 | tf_op jit(solution)/shard_map/mik,mjk->mij/dot_general | solution.py:21
  228.0 0.0 all-reduce.5.cloned.1.call-update
  228.1 0.3 all-reduce.7.cloned.1.call-start
  228.3 29.1 %all-reduce.5.cloned.1.call-done = f32[8,128,128]{2,1,0:T(8,128)} async-done(((f32[8,128,128]{2,1,0:T(8,128)}), f32[8,128,128]{2,1,0:T(8,128)}) %all-reduce.5.cloned.1.call-update) | async-done | bytes 524304 | tf_op jit(solution)/shard_map/psum | solution.py:20
  257.4 2.1 fusion.7
  259.5 11.7 %multiply_add_fusion.3 = f32[8,128,2048]{2,1,0:T(8,128)S(1)} fusion(f32[8,128,128]{2,1,0:T(8,128)S(1)} %fusion.7, f32[8]{0:T(128)S(1)} %rsqrt_bitcast_fusion, f32[16,8,8,2048]{3,2,1,0:T(8,128)} %copy-done), kind=kOutput, calls=%fused_computation.5 | convolution fusion | flops 3229614080 | bytes 17301536 | tf_op jit(solution)/shard_map/mij,mjk->mik/dot_general | solution.py:26
  271.3 0.0 copy-start.1
  271.3 3.4 copy-done.1
  274.7 8.5 %fusion.24 = f32[8,128,128]{2,1,0:T(8,128)} fusion(f32[8,128,2048]{2,1,0:T(8,128)S(1)} %multiply_add_fusion.3), kind=kOutput, calls=%fused_computation.55 | convolution fusion | flops 3221225472 | bytes 8912896 | tf_op jit(solution)/shard_map/mik,mjk->mij/dot_general | solution.py:21
  283.2 0.0 all-reduce.7.cloned.1.call-update
  283.2 0.0 all-reduce.9.cloned.1.call-start
  283.3 28.8 %all-reduce.7.cloned.1.call-done = f32[8,128,128]{2,1,0:T(8,128)} async-done(((f32[8,128,128]{2,1,0:T(8,128)}), f32[8,128,128]{2,1,0:T(8,128)}) %all-reduce.7.cloned.1.call-update) | async-done | bytes 524304 | tf_op jit(solution)/shard_map/psum | solution.py:20
  312.0 2.1 fusion.6
  314.1 14.4 %multiply_add_fusion.2 = f32[8,128,2048]{2,1,0:T(8,128)S(1)} fusion(f32[8,128,2048]{2,1,0:T(8,128)} %copy-done.1, f32[8,128,128]{2,1,0:T(8,128)S(1)} %fusion.6), kind=kOutput, calls=%fused_computation.4 | convolution fusion | flops 3225419776 | bytes 17301504 | tf_op jit(solution)/shard_map/mij,mjk->mik/dot_general | solution.py:26
  328.5 0.0 copy-start.2
  328.5 3.4 copy-done.2
  331.9 8.5 %fusion.25 = f32[8,128,128]{2,1,0:T(8,128)} fusion(f32[8,128,2048]{2,1,0:T(8,128)S(1)} %multiply_add_fusion.2), kind=kOutput, calls=%fused_computation.56 | convolution fusion | flops 3221225472 | bytes 8912896 | tf_op jit(solution)/shard_map/mik,mjk->mij/dot_general | solution.py:21
  340.4 0.0 all-reduce.9.cloned.1.call-update
  340.5 0.0 all-reduce.11.cloned.1.call-start
  340.5 28.7 %all-reduce.9.cloned.1.call-done = f32[8,128,128]{2,1,0:T(8,128)} async-done(((f32[8,128,128]{2,1,0:T(8,128)}), f32[8,128,128]{2,1,0:T(8,128)}) %all-reduce.9.cloned.1.call-update) | async-done | bytes 524304 | tf_op jit(solution)/shard_map/psum | solution.py:20
  369.3 2.1 fusion.5
  371.3 14.1 %multiply_add_fusion.1 = f32[8,128,2048]{2,1,0:T(8,128)S(1)} fusion(f32[8,128,2048]{2,1,0:T(8,128)} %copy-done.2, f32[8,128,128]{2,1,0:T(8,128)S(1)} %fusion.5), kind=kOutput, calls=%fused_computation.3 | convolution fusion | flops 3225419776 | bytes 17301504 | tf_op jit(solution)/shard_map/mij,mjk->mik/dot_general | solution.py:26
  385.4 0.0 copy-start.3
  385.5 3.4 copy-done.3
  388.9 8.5 %fusion.26 = f32[8,128,128]{2,1,0:T(8,128)} fusion(f32[8,128,2048]{2,1,0:T(8,128)S(1)} %multiply_add_fusion.1), kind=kOutput, calls=%fused_computation.57 | convolution fusion | flops 3221225472 | bytes 8912896 | tf_op jit(solution)/shard_map/mik,mjk->mij/dot_general | solution.py:21
  397.4 0.0 all-reduce.11.cloned.1.call-update
  397.4 28.8 %all-reduce.11.cloned.1.call-done = f32[8,128,128]{2,1,0:T(8,128)} async-done(((f32[8,128,128]{2,1,0:T(8,128)}), f32[8,128,128]{2,1,0:T(8,128)}) %all-reduce.11.cloned.1.call-update) | async-done | bytes 524304 | tf_op jit(solution)/shard_map/psum | solution.py:20
  426.2 2.1 fusion.4
  428.3 14.9 %multiply_add_fusion = f32[8,128,2048]{2,1,0:T(8,128)S(1)} fusion(f32[8,128,2048]{2,1,0:T(8,128)} %copy-done.3, f32[8,128,128]{2,1,0:T(8,128)S(1)} %fusion.4), kind=kOutput, calls=%fused_computation.2 | convolution fusion | flops 3225419776 | bytes 17301504 | tf_op jit(solution)/shard_map/mij,mjk->mik/dot_general | solution.py:26
  443.1 4.9 copy.8
  448.0 188.9 %all_to_all.15 = f32[8,128,2048]{2,0,1:T(8,128)S(1)} all-to-all(f32[8,128,2048]{2,0,1:T(8,128)S(1)} %copy.8), channel_id=1, replica_groups=mesh['shard'=16,'model'=2] {'shard'}, dimensions={1} | all-to-all | bytes 16777216 | tf_op jit(solution)/shard_map/all_to_all | solution.py:29
  637.0 1.8 broadcast_multiply_fusion
  638.8 9.7 %copy.9 = f32[16,8,8,2048]{3,2,1,0:T(8,128)} copy(f32[16,8,8,2048]{3,1,2,0:T(8,128)S(1)} %bitcast.110) | data formatting | bytes 16777216 | tf_op jit(solution)/shard_map/mul | solution.py:30
  648.5 11.9 %bitcast_subtract_fusion = f32[128,8,2048]{2,1,0:T(8,128)} fusion(f32[128,8,2048]{2,1,0:T(8,128)} %param.5, f32[16,8,8,2048]{3,2,1,0:T(8,128)} %copy.9), kind=kLoop, calls=%fused_computation | loop fusion | flops 2097152 | bytes 25165824 | tf_op jit(solution)/shard_map/sub | solution.py:30
  (17 shorter events, 0.6 us)
Async XLA Ops:
  7.2 250.3 %all-reduce.5.cloned.1.call-start = ((), (), s32[]{:S(2)}) async-start(), calls=%async_computation.2 | async-start | bytes 1048576 | tf_op jit(solution)/shard_map/psum | solution.py:20
  206.9 3.4 copy-start
  228.1 84.0 %all-reduce.7.cloned.1.call-start = ((), (), s32[]{:S(2)}) async-start(), calls=%async_computation.3 | async-start | bytes 1048576 | tf_op jit(solution)/shard_map/psum | solution.py:20
  271.3 3.4 copy-start.1
  283.2 86.0 %all-reduce.9.cloned.1.call-start = ((), (), s32[]{:S(2)}) async-start(), calls=%async_computation.4 | async-start | bytes 1048576 | tf_op jit(solution)/shard_map/psum | solution.py:20
  328.5 3.4 copy-start.2
  340.5 85.7 %all-reduce.11.cloned.1.call-start = ((), (), s32[]{:S(2)}) async-start(), calls=%async_computation.5 | async-start | bytes 1048576 | tf_op jit(solution)/shard_map/psum | solution.py:20
  385.4 3.4 copy-start.3
Sparse Core Ops, SparseCore 0:
  228.2 29.1 all-reduce.4
  283.3 28.6 all-reduce.6
  340.6 28.6 all-reduce.8
  397.5 28.6 all-reduce.10
